TPU v7x, 32 devices: a whole 2x2x4 slice. The times are simulated.
32 devices in a mesh: dom: 8 (over y, x, core), orb: 4 (over z).
Axes of the slice: x: 2, y: 2, z: 4, core: 2. Of those that a mesh axis runs over, the one named last changes fastest.
Arguments:
- orbitals: float32 [8, 64, 64, 128], P('orb', 'dom'), may hold values from -10.8 to 10.8
- initial_guess: float32 [8, 64, 64, 128], P('orb', 'dom'), may hold values from -350 to 350
- potential: float32 [64, 64, 128], P('dom'), may hold values from 0.1 to 2
- perturbation: float32 [64, 64, 128], P('dom'), may hold values from -6 to 6
- level_shifts: float32 [8], replicated, may hold values from 0.05 to 2
- assignment: int32 [8], P('orb'), may hold values from 0 to 7, each once
Outputs:
- updated_response: float32 [8, 64, 64, 128], P('orb', 'dom')
Inputs may be any that keep to these rules, and one draw needn't show every extreme that they name: `assignment`: every energy index appears in exactly one slot.
All inputs are finite; a program needn't handle non-finite values.
Results may differ from a plain program's by a relative error of at most 0.0003.
Values sent between devices are 32-bit elements; how exact they have to be, the bound alone decides.
No kernel may reach another device: no remote copies, remote signals or barrier semaphores. Data moves between devices by JAX's collectives and lax.ppermute only.
A program may use at most 128 MiB of HBM per device.

v0:
```python
import jax
import jax.numpy as jnp
from jax import lax
from jax.sharding import PartitionSpec as P

SWEEPS = 2
COARSE = 4
OMEGA = 0.8
KINETIC = 8.0


def with_halo(block, sides, width):
    for axis, dim in sides:
        count = lax.axis_size(axis)
        forward = [(i, i + 1) for i in range(count - 1)]
        forward.append((count - 1, 0))
        backward = [(target, source) for source, target in forward]
        low = lax.ppermute(
            lax.slice_in_dim(block, block.shape[dim] - width, None, axis=dim), axis, forward
        )
        high = lax.ppermute(lax.slice_in_dim(block, 0, width, axis=dim), axis, backward)
        block = jnp.concatenate([low, block, high], axis=dim)
    return block


def apply_level(field_values, potential_level, shift_column, level, padded):
    inverse_area = 0.25**level
    plus_x = padded[:, 2:]
    minus_x = padded[:, :-2]
    neighbours = (
        plus_x
        + minus_x
        + (jnp.roll(field_values, -1, 2) + jnp.roll(field_values, 1, 2))
        + (jnp.roll(field_values, -1, 3) + jnp.roll(field_values, 1, 3))
    )
    return (
        KINETIC * inverse_area * (6.0 * field_values - neighbours)
        + (potential_level + shift_column) * field_values
    )


def diagonal_of(potential_level, shift_column, level):
    return 6.0 * KINETIC * 0.25**level + potential_level + shift_column


def relax(estimate, source, potential_level, shift_column, level, padded):
    applied = apply_level(estimate, potential_level, shift_column, level, padded)
    return estimate + OMEGA * (source - applied) / diagonal_of(potential_level, shift_column, level)


def coarsen(field_values):
    lead, sx, sy, sz = field_values.shape
    return field_values.reshape(lead, sx // 2, 2, sy // 2, 2, sz // 2, 2).mean(axis=(2, 4, 6))


def refine(field_values):
    return jnp.repeat(jnp.repeat(jnp.repeat(field_values, 2, 1), 2, 2), 2, 3)


def fine_pad(field_values):
    return with_halo(field_values, (("dom", 1),), 1)


def middle_pad(field_values):
    return with_halo(field_values, (("dom", 1),), 1)


def on_device(orbitals, initial_guess, potential, perturbation, level_shifts, assignment):
    local_count = orbitals.shape[0]
    total_orbitals = level_shifts.shape[0]
    onehot = (assignment[:, None] == jnp.arange(total_orbitals, dtype=jnp.int32)[None, :]).astype(
        jnp.float32
    )
    shifts = jnp.sum(onehot * level_shifts[None, :], axis=1)
    shift_column = shifts[:, None, None, None]
    levels = [potential[None]]
    levels.append(coarsen(levels[0]))
    levels.append(coarsen(levels[1]))
    pads = [fine_pad, middle_pad]
    source = -(perturbation[None] * orbitals)
    sources = [
        source - apply_level(initial_guess, levels[0], shift_column, 0, fine_pad(initial_guess))
    ]
    estimates = []
    for level in range(2):
        current = sources[level]
        estimate = OMEGA * current / diagonal_of(levels[level], shift_column, level)
        estimate = relax(
            estimate, current, levels[level], shift_column, level, pads[level](estimate)
        )
        remainder = current - apply_level(
            estimate, levels[level], shift_column, level, pads[level](estimate)
        )
        estimates.append(estimate)
        sources.append(coarsen(remainder))
    lower = OMEGA * sources[2] / diagonal_of(levels[2], shift_column, 2)
    for sweep_index in range(COARSE - 1):
        padded = with_halo(lower, (("dom", 1),), 1)
        lower = relax(lower, sources[2], levels[2], shift_column, 2, padded)
    for level in (1, 0):
        estimate = estimates[level] + refine(lower)
        for sweep_index in range(SWEEPS):
            estimate = relax(
                estimate, sources[level], levels[level], shift_column, level, pads[level](estimate)
            )
        lower = estimate
    update = initial_guess + lower
    cells_total = orbitals.shape[1] * lax.axis_size("dom") * orbitals.shape[2] * orbitals.shape[3]
    everyone = lax.all_gather(orbitals, "orb", axis=0, tiled=True)
    flat_orbit = everyone.reshape(total_orbitals, -1)
    flat_update = update.reshape(local_count, -1)
    partial_intersection = jnp.einsum(
        "jc,ic->ji", flat_orbit, flat_update, precision=lax.Precision.HIGHEST
    )
    intersection = lax.psum(partial_intersection, "dom") / cells_total
    corrected = flat_update - jnp.einsum(
        "ji,jc->ic", intersection, flat_orbit, precision=lax.Precision.HIGHEST
    )
    result = corrected.reshape(update.shape)
    return result


def solution(mesh):
    in_specs = (
        P("orb", "dom", None, None),
        P("orb", "dom", None, None),
        P("dom", None, None),
        P("dom", None, None),
        P(),
        P("orb"),
    )
    out_specs = P("orb", "dom", None, None)
    return jax.shard_map(
        on_device, mesh=mesh, in_specs=in_specs, out_specs=out_specs, check_vma=False
    )
```

profile of v0, /device:TPU:0, one launch (start us, length us, event | category | flops | bytes accessed | tf_op | source)
XLA Modules:
  0.0 242.5 jit_solution(13926288601825531466)
XLA Ops:
  6.5 0.9 fusion.140
  7.4 3.4 %collective-permute-start = (f32[2,1,64,128]{3,2,1,0:T(8,128)S(1)}, f32[2,1,64,128]{3,2,1,0:T(8,128)S(1)}, u32[]{:S(2)}, u32[]{:S(2)}) collective-permute-start(f32[2,1,64,128]{3,2,1,0:T(8,128)S(1)} %get-tuple-element.56), channel_id=1, source_target_pairs={{4,0},{8,4},{12,8},{16,12},{20,16},{24,20},{28,24},{0,28},{5,1},{9... | collective-permute-start | bytes 196616 | tf_op jit(solution)/shard_map/ppermute | solution.py:21
  10.9 1.4 copy.131
  12.3 1.6 fusion.137
  13.9 1.5 fusion.138
  16.4 1.3 copy.111
  17.7 18.1 %reshape_broadcast_in_dim.3 = f32[4,2,32,2,64,2]{5,4,3,2,1,0:T(8,128)} reshape(f32[8,64,128]{2,1,0:T(8,128)S(1)} %copy-done.9) | data formatting | bytes 524288 | tf_op jit(solution)/shard_map/reshape;broadcast_in_dim | solution.py:53
  36.0 1.4 copy.116
  37.4 1.4 copy.118
  38.8 1.0 copy.110
  39.8 7.1 %reduce_sum.47 = f32[4,32,64]{2,1,0:T(8,128)S(1)} reduce(f32[4,2,32,2,64,2]{5,4,3,2,1,0:T(8,128)} %reshape_broadcast_in_dim.3, f32[]{:T(128)} %constant.14.clone.1), dimensions={1,3,5}, to_apply=%region_2.0 | reduce | flops 57344 | bytes 294916 | tf_op jit(solution)/shard_map/reduce_sum | solution.py:53
  46.9 3.5 %div.73 = f32[2,2,16,2,32,2]{5,4,3,2,1,0:T(8,128)} reshape(f32[4,32,64]{2,1,0:T(8,128)S(1)} %get-tuple-element.99) | data formatting | bytes 65536 | tf_op jit(solution)/shard_map/div | solution.py:53
  50.4 1.8 reduce_sum.49
  53.0 1.8 pad_maximum_fusion.8
  54.8 2.3 copy.136
  57.1 1.4 copy.137
  58.6 4.9 %add_divide_fusion.3 = (f32[2,8,64,128]{2,1,3,0:T(8,128)S(1)}, f32[2,8,64,128]{2,1,3,0:T(8,128)S(1)}) fusion(f32[8,64,128]{1,0,2:T(8,128)S(1)} %copy.125, f32[2]{0:T(128)S(1)} %fusion.112, f32[2,8,64,128]{2,1,3,0:T(8,128)S(1)} %copy.131, f32[8,64,128]{1,0,2:T(8,128)S(1)} %copy.123, f32[2,8,64,127]{2,1,3,0:T(8,128)} %get-tuple-element.50, ...), kind=kLoop, calls=%fused_computation.9 | loop fusion | flops 2752512 | bytes 6029320 | tf_op jit(solution)/shard_map/div | solution.py:87
  64.4 2.7 %collective-permute-start.2 = (f32[2,1,64,128]{2,1,3,0:T(1,128)S(1)}, f32[2,1,64,128]{2,1,3,0:T(1,128)S(1)}, u32[]{:S(2)}, u32[]{:S(2)}) collective-permute-start(f32[2,1,64,128]{2,1,3,0:T(1,128)S(1)} %get-tuple-element.45), channel_id=1, source_target_pairs={{4,0},{8,4},{12,8},{16,12},{20,16},{24,20},{28,24},{0,28},{5,1},{9... | collective-permute-start | bytes 196616 | tf_op jit(solution)/shard_map/ppermute | solution.py:21
  67.1 2.5 %collective-permute-done.2 = f32[2,1,64,128]{2,1,3,0:T(1,128)S(1)} collective-permute-done((f32[2,1,64,128]{2,1,3,0:T(1,128)S(1)}, f32[2,1,64,128]{2,1,3,0:T(1,128)S(1)}, u32[]{:S(2)}, u32[]{:S(2)}) %collective-permute-start.2) | collective-permute-done | bytes 65568 | tf_op jit(solution)/shard_map/ppermute | solution.py:21
  69.7 2.8 %collective-permute-done.3 = f32[2,1,64,128]{2,1,3,0:T(1,128)S(1)} collective-permute-done((f32[2,1,64,128]{2,1,3,0:T(1,128)S(1)}, f32[2,1,64,128]{2,1,3,0:T(1,128)S(1)}, u32[]{:S(2)}, u32[]{:S(2)}) %collective-permute-start.3) | collective-permute-done | bytes 65568 | tf_op jit(solution)/shard_map/ppermute | solution.py:18
  72.4 1.4 fusion.10
  75.4 3.2 %collective-permute-done.4 = f32[2,1,64,128]{2,1,3,0:T(1,128)S(1)} collective-permute-done((f32[2,1,64,128]{2,1,3,0:T(1,128)S(1)}, f32[2,1,64,128]{2,1,3,0:T(1,128)S(1)}, u32[]{:S(2)}, u32[]{:S(2)}) %collective-permute-start.4) | collective-permute-done | bytes 65568 | tf_op jit(solution)/shard_map/ppermute | solution.py:21
  78.6 1.8 collective-permute-done.5
  80.4 2.2 fusion.20
  82.7 2.3 copy.126
  85.0 35.6 %reshape.71 = f32[2,4,2,32,2,64,2]{6,5,4,3,2,1,0:T(8,128)} reshape(f32[2,8,64,128]{3,2,1,0:T(8,128)} %copy.126) | data formatting | bytes 1048576 | tf_op jit(solution)/shard_map/reshape | solution.py:53
  120.6 12.2 %reduce_sum.46 = f32[2,4,32,64]{3,2,1,0:T(8,128)S(1)} reduce(f32[2,4,2,32,2,64,2]{6,5,4,3,2,1,0:T(8,128)} %reshape.71, f32[]{:T(128)} %constant.14.clone.1), dimensions={2,4,6}, to_apply=%region_1.0 | reduce | flops 114688 | bytes 589828 | tf_op jit(solution)/shard_map/reduce_sum | solution.py:53
  133.2 1.0 collective-permute-start.6
  134.2 1.6 collective-permute-done.6
  135.8 2.6 %collective-permute-done.7 = f32[2,1,32,64]{3,2,1,0:T(8,128)S(1)} collective-permute-done((f32[2,1,32,64]{3,2,1,0:T(8,128)S(1)}, f32[2,1,32,64]{3,2,1,0:T(8,128)S(1)}, u32[]{:S(2)}, u32[]{:S(2)}) %collective-permute-start.7) | collective-permute-done | bytes 16416 | tf_op jit(solution)/shard_map/ppermute | solution.py:18
  140.1 1.1 collective-permute-done.8
  141.2 2.7 %collective-permute-done.9 = f32[2,1,32,64]{3,2,1,0:T(8,128)S(1)} collective-permute-done((f32[2,1,32,64]{3,2,1,0:T(8,128)S(1)}, f32[2,1,32,64]{3,2,1,0:T(8,128)S(1)}, u32[]{:S(2)}, u32[]{:S(2)}) %collective-permute-start.9) | collective-permute-done | bytes 16416 | tf_op jit(solution)/shard_map/ppermute | solution.py:18
  144.7 6.5 %reshape.72 = f32[2,2,2,16,2,32,2]{6,5,4,3,2,1,0:T(8,128)} reshape(f32[2,4,32,64]{3,2,1,0:T(8,128)} %fusion.58) | data formatting | bytes 131072 | tf_op jit(solution)/shard_map/reshape | solution.py:53
  151.2 3.2 %reduce_sum.48 = f32[2,2,16,32]{3,2,1,0:T(8,128)} reduce(f32[2,2,2,16,2,32,2]{6,5,4,3,2,1,0:T(8,128)} %reshape.72, f32[]{:T(128)} %constant.14.clone.1), dimensions={2,4,6}, to_apply=%region_3.4 | reduce | flops 14336 | bytes 73732 | tf_op jit(solution)/shard_map/reduce_sum | solution.py:53
  154.4 0.9 add_divide_fusion.11
  156.0 1.0 collective-permute-done.10
  157.1 2.6 %collective-permute-done.11 = f32[2,1,16,32]{3,2,1,0:T(8,128)S(1)} collective-permute-done((f32[2,1,16,32]{3,2,1,0:T(8,128)S(1)}, f32[2,1,16,32]{3,2,1,0:T(8,128)S(1)}, u32[]{:S(2)}, u32[]{:S(2)}) %collective-permute-start.11) | collective-permute-done | bytes 4128 | tf_op jit(solution)/shard_map/ppermute | solution.py:18
  159.7 0.9 fusion.88
  161.3 0.9 collective-permute-done.12
  162.3 2.7 %collective-permute-done.13 = f32[2,1,16,32]{3,2,1,0:T(8,128)S(1)} collective-permute-done((f32[2,1,16,32]{3,2,1,0:T(8,128)S(1)}, f32[2,1,16,32]{3,2,1,0:T(8,128)S(1)}, u32[]{:S(2)}, u32[]{:S(2)}) %collective-permute-start.13) | collective-permute-done | bytes 4128 | tf_op jit(solution)/shard_map/ppermute | solution.py:18
  166.6 0.9 collective-permute-done.14
  167.5 2.7 %collective-permute-done.15 = f32[2,1,16,32]{3,2,1,0:T(8,128)S(1)} collective-permute-done((f32[2,1,16,32]{3,2,1,0:T(8,128)S(1)}, f32[2,1,16,32]{3,2,1,0:T(8,128)S(1)}, u32[]{:S(2)}, u32[]{:S(2)}) %collective-permute-start.15) | collective-permute-done | bytes 4128 | tf_op jit(solution)/shard_map/ppermute | solution.py:18
  171.0 1.6 copy.127
  172.7 1.7 broadcast_in_dim.26
  174.4 1.7 copy.128
  176.1 0.9 add.552
  177.8 1.1 collective-permute-done.16
  178.9 2.7 %collective-permute-done.17 = f32[2,1,32,64]{3,2,1,0:T(8,128)S(1)} collective-permute-done((f32[2,1,32,64]{3,2,1,0:T(8,128)S(1)}, f32[2,1,32,64]{3,2,1,0:T(8,128)S(1)}, u32[]{:S(2)}, u32[]{:S(2)}) %collective-permute-start.17) | collective-permute-done | bytes 16416 | tf_op jit(solution)/shard_map/ppermute | solution.py:18
  183.3 1.2 collective-permute-done.18
  184.5 2.6 %collective-permute-done.19 = f32[2,1,32,64]{3,2,1,0:T(8,128)S(1)} collective-permute-done((f32[2,1,32,64]{3,2,1,0:T(8,128)S(1)}, f32[2,1,32,64]{3,2,1,0:T(8,128)S(1)}, u32[]{:S(2)}, u32[]{:S(2)}) %collective-permute-start.19) | collective-permute-done | bytes 16416 | tf_op jit(solution)/shard_map/ppermute | solution.py:18
  188.3 2.1 copy.130
  190.4 1.1 broadcast_in_dim.29
  193.2 2.7 %collective-permute-done.20 = f32[2,1,64,128]{2,1,3,0:T(1,128)S(1)} collective-permute-done((f32[2,1,64,128]{2,1,3,0:T(1,128)S(1)}, f32[2,1,64,128]{2,1,3,0:T(1,128)S(1)}, u32[]{:S(2)}, u32[]{:S(2)}) %collective-permute-start.20) | collective-permute-done | bytes 65568 | tf_op jit(solution)/shard_map/ppermute | solution.py:21
  195.9 1.6 collective-permute-done.21
  197.5 1.4 fusion.11
  199.1 1.4 collective-permute-start.22
  201.4 2.0 collective-permute-done.22
  203.4 2.5 %collective-permute-done.23 = f32[2,1,64,128]{2,1,3,0:T(1,128)S(1)} collective-permute-done((f32[2,1,64,128]{2,1,3,0:T(1,128)S(1)}, f32[2,1,64,128]{2,1,3,0:T(1,128)S(1)}, u32[]{:S(2)}, u32[]{:S(2)}) %collective-permute-start.23) | collective-permute-done | bytes 65568 | tf_op jit(solution)/shard_map/ppermute | solution.py:18
  205.9 2.4 fusion.13
  208.2 2.4 %copy.133 = f32[2,8,64,128]{3,0,2,1:T(2,128)} copy(f32[2,8,64,128]{2,1,3,0:T(8,128)} %fusion.13) | data formatting | bytes 1048576 | tf_op jit(solution)/shard_map/add | solution.py:107
  210.7 6.7 %fusion.7 = f32[8,2]{0,1:T(2,128)S(1)} fusion(f32[2,8,64,128]{3,0,2,1:T(2,128)} %copy.133, f32[8,8,64,128]{3,2,1,0:T(8,128)} %all-gather.2.cloned.1.call-done), kind=kOutput, calls=%fused_computation.15 | convolution fusion | flops 12582912 | bytes 2621504 | tf_op jit(solution)/shard_map/jc,ic->ji/dot_general | solution.py:112
  217.4 1.2 copy.132
  218.6 12.1 %psum.7 = f32[8,2]{0,1:T(2,128)S(1)} all-reduce(f32[8,2]{0,1:T(2,128)S(1)} %fusion.7), channel_id=1, replica_groups=mesh['dom'=8,'orb'=4] {'dom'}, use_global_device_ids=true, to_apply=%region_5.6 | all-reduce | flops 16 | bytes 128 | tf_op jit(solution)/shard_map/psum | solution.py:115
  230.7 4.1 %fusion.4 = f32[1,2,512,128]{3,1,2,0:T(2,128)S(1)} fusion(f32[1,8,512,128]{3,2,1,0:T(8,128)S(1)} %bitcast.32, f32[1,2,512,128]{3,2,1,0:T(8,128)} %bitcast.34, f32[8,2]{0,1:T(2,128)S(1)} %psum.7), kind=kOutput, calls=%fused_computation.14 | convolution fusion | flops 12714000 | bytes 3145792 | tf_op jit(solution)/shard_map/ji,jc->ic/dot_general | solution.py:116
  (146 shorter events, 18.2 us)
Async XLA Ops:
  6.5 204.1 %all-gather.2.cloned.1.call-start = ((), (), s32[]{:S(2)}) async-start(), calls=%async_computation | async-start | bytes 2621440 | tf_op jit(solution)/shard_map/all_gather | solution.py:109
  7.4 45.6 %collective-permute-start = (f32[2,1,64,128]{3,2,1,0:T(8,128)S(1)}, f32[2,1,64,128]{3,2,1,0:T(8,128)S(1)}, u32[]{:S(2)}, u32[]{:S(2)}) collective-permute-start(f32[2,1,64,128]{3,2,1,0:T(8,128)S(1)} %get-tuple-element.56), channel_id=1, source_target_pairs={{4,0},{8,4},{12,8},{16,12},{20,16},{24,20},{28,24},{0,28},{5,1},{9... | collective-permute-start | bytes 196616 | tf_op jit(solution)/shard_map/ppermute | solution.py:21
  10.8 42.2 %collective-permute-start.1 = (f32[2,1,64,128]{3,2,1,0:T(8,128)S(1)}, f32[2,1,64,128]{3,2,1,0:T(8,128)}, u32[]{:S(2)}, u32[]{:S(2)}) collective-permute-start(f32[2,1,64,128]{3,2,1,0:T(8,128)S(1)} %get-tuple-element.55), channel_id=1, source_target_pairs={{0,4},{4,8},{8,12},{12,16},{16,20},{20,24},{24,28},{28,0},{1,5},{5... | collective-permute-start | bytes 196616 | tf_op jit(solution)/shard_map/ppermute | solution.py:18
  13.9 2.1 copy-start.9
  13.9 2.4 copy-start.8
  13.9 2.4 %copy-start.10 = (f32[2,8,64,128]{3,2,1,0:T(8,128)S(1)}, f32[2,8,64,128]{3,2,1,0:T(8,128)}, u32[]{:S(2)}) copy-start(f32[2,8,64,128]{3,2,1,0:T(8,128)} %param.6) | copy-start | bytes 1572868
  16.3 42.2 %copy-start = (f32[8,64,128]{1,0,2:T(8,128)}, f32[8,64,128]{1,0,2:T(8,128)S(1)}, u32[]{:S(2)}) copy-start(f32[8,64,128]{1,0,2:T(8,128)S(1)} %copy.123) | copy-start | bytes 786436
  35.7 3.0 %copy-start.12 = (f32[8,64,128]{2,1,0:T(8,128)S(1)}, f32[8,64,128]{2,1,0:T(8,128)}, u32[]{:S(2)}) copy-start(f32[8,64,128]{2,1,0:T(8,128)} %param.9) | copy-start | bytes 786436
  36.0 22.5 %copy-start.3 = (f32[8,64,128]{1,0,2:T(8,128)}, f32[8,64,128]{1,0,2:T(8,128)S(1)}, u32[]{:S(2)}) copy-start(f32[8,64,128]{1,0,2:T(8,128)S(1)} %copy.125) | copy-start | bytes 786436
  46.9 5.9 %copy-start.20 = (f32[8]{0:T(128)S(1)}, f32[8]{0:T(128)}, u32[]{:S(2)}) copy-start(f32[8]{0:T(128)} %param.10) | copy-start | bytes 100
  46.9 5.9 %copy-start.21 = (s32[2]{0:T(128)S(1)}, s32[2]{0:T(128)}, u32[]{:S(2)}) copy-start(s32[2]{0:T(128)} %param.11) | copy-start | bytes 28
  53.0 79.9 %copy-start.14 = (f32[2]{0:T(128)}, f32[2]{0:T(128)S(1)}, u32[]{:S(2)}) copy-start(f32[2]{0:T(128)S(1)} %fusion.112) | copy-start | bytes 28
  53.0 5.6 %copy-start.18 = (f32[2,8,64,1]{2,1,3,0:T(8,128)S(1)}, f32[2,8,64,1]{2,1,3,0:T(8,128)}, u32[]{:S(2)}) copy-start(f32[2,8,64,1]{2,1,3,0:T(8,128)} %get-tuple-element.51) | copy-start | bytes 12292
  53.0 5.6 %copy-start.19 = (f32[2,8,64,1]{2,1,3,0:T(8,128)S(1)}, f32[2,8,64,1]{2,1,3,0:T(8,128)}, u32[]{:S(2)}) copy-start(f32[2,8,64,1]{2,1,3,0:T(8,128)} %get-tuple-element.52) | copy-start | bytes 12292
  64.1 8.3 %copy-start.1 = (f32[8,64,128]{1,0,2:T(8,128)S(1)}, f32[8,64,128]{1,0,2:T(8,128)}, u32[]{:S(2)}) copy-start(f32[8,64,128]{1,0,2:T(8,128)} %copy-done) | copy-start | bytes 786436
  64.1 8.3 %copy-start.4 = (f32[8,64,128]{1,0,2:T(8,128)S(1)}, f32[8,64,128]{1,0,2:T(8,128)}, u32[]{:S(2)}) copy-start(f32[8,64,128]{1,0,2:T(8,128)} %copy-done.3) | copy-start | bytes 786436
  64.4 5.2 %collective-permute-start.2 = (f32[2,1,64,128]{2,1,3,0:T(1,128)S(1)}, f32[2,1,64,128]{2,1,3,0:T(1,128)S(1)}, u32[]{:S(2)}, u32[]{:S(2)}) collective-permute-start(f32[2,1,64,128]{2,1,3,0:T(1,128)S(1)} %get-tuple-element.45), channel_id=1, source_target_pairs={{4,0},{8,4},{12,8},{16,12},{20,16},{24,20},{28,24},{0,28},{5,1},{9... | collective-permute-start | bytes 196616 | tf_op jit(solution)/shard_map/ppermute | solution.py:21
  67.1 5.3 %collective-permute-start.3 = (f32[2,1,64,128]{2,1,3,0:T(1,128)S(1)}, f32[2,1,64,128]{2,1,3,0:T(1,128)S(1)}, u32[]{:S(2)}, u32[]{:S(2)}) collective-permute-start(f32[2,1,64,128]{2,1,3,0:T(1,128)S(1)} %get-tuple-element.46), channel_id=1, source_target_pairs={{0,4},{4,8},{8,12},{12,16},{16,20},{20,24},{24,28},{28,0},{1,5},{5... | collective-permute-start | bytes 196616 | tf_op jit(solution)/shard_map/ppermute | solution.py:18
  74.8 3.8 %collective-permute-start.4 = (f32[2,1,64,128]{2,1,3,0:T(1,128)S(1)}, f32[2,1,64,128]{2,1,3,0:T(1,128)S(1)}, u32[]{:S(2)}, u32[]{:S(2)}) collective-permute-start(f32[2,1,64,128]{2,1,3,0:T(1,128)S(1)} %get-tuple-element.35), channel_id=1, source_target_pairs={{4,0},{8,4},{12,8},{16,12},{20,16},{24,20},{28,24},{0,28},{5,1},{9... | collective-permute-start | bytes 196616 | tf_op jit(solution)/shard_map/ppermute | solution.py:21
  74.9 5.5 %collective-permute-start.5 = (f32[2,1,64,128]{2,1,3,0:T(1,128)S(1)}, f32[2,1,64,128]{2,1,3,0:T(1,128)S(1)}, u32[]{:S(2)}, u32[]{:S(2)}) collective-permute-start(f32[2,1,64,128]{2,1,3,0:T(1,128)S(1)} %get-tuple-element.36), channel_id=1, source_target_pairs={{0,4},{4,8},{8,12},{12,16},{16,20},{20,24},{24,28},{28,0},{1,5},{5... | collective-permute-start | bytes 196616 | tf_op jit(solution)/shard_map/ppermute | solution.py:18
  133.0 10.8 %copy-start.15 = (f32[2]{0:T(128)S(1)}, f32[2]{0:T(128)}, u32[]{:S(2)}) copy-start(f32[2]{0:T(128)} %copy-done.14) | copy-start | bytes 28
  133.2 2.6 %collective-permute-start.6 = (f32[2,1,32,64]{3,2,1,0:T(8,128)S(1)}, f32[2,1,32,64]{3,2,1,0:T(8,128)S(1)}, u32[]{:S(2)}, u32[]{:S(2)}) collective-permute-start(f32[2,1,32,64]{3,2,1,0:T(8,128)S(1)} %get-tuple-element.97), channel_id=1, source_target_pairs={{4,0},{8,4},{12,8},{16,12},{20,16},{24,20},{28,24},{0,28},{5,1},{9... | collective-permute-start | bytes 49160 | tf_op jit(solution)/shard_map/ppermute | solution.py:21
  134.2 4.2 %collective-permute-start.7 = (f32[2,1,32,64]{3,2,1,0:T(8,128)S(1)}, f32[2,1,32,64]{3,2,1,0:T(8,128)S(1)}, u32[]{:S(2)}, u32[]{:S(2)}) collective-permute-start(f32[2,1,32,64]{3,2,1,0:T(8,128)S(1)} %get-tuple-element.98), channel_id=1, source_target_pairs={{0,4},{4,8},{8,12},{12,16},{16,20},{20,24},{24,28},{28,0},{1,5},{5... | collective-permute-start | bytes 49160 | tf_op jit(solution)/shard_map/ppermute | solution.py:18
  139.5 1.7 collective-permute-start.8
  139.6 4.3 %collective-permute-start.9 = (f32[2,1,32,64]{3,2,1,0:T(8,128)S(1)}, f32[2,1,32,64]{3,2,1,0:T(8,128)S(1)}, u32[]{:S(2)}, u32[]{:S(2)}) collective-permute-start(f32[2,1,32,64]{3,2,1,0:T(8,128)S(1)} %get-tuple-element.88), channel_id=1, source_target_pairs={{0,4},{4,8},{8,12},{12,16},{16,20},{20,24},{24,28},{28,0},{1,5},{5... | collective-permute-start | bytes 49160 | tf_op jit(solution)/shard_map/ppermute | solution.py:18
  154.4 15.8 %copy-start.11 = (f32[2,2,16,32]{3,2,1,0:T(8,128)S(1)}, f32[2,2,16,32]{3,2,1,0:T(8,128)}, u32[]{:S(2)}) copy-start(f32[2,2,16,32]{3,2,1,0:T(8,128)} %reduce_sum.48) | copy-start | bytes 24580
  154.4 15.8 %copy-start.13 = (f32[2,16,32]{2,1,0:T(8,128)S(1)}, f32[2,16,32]{2,1,0:T(8,128)}, u32[]{:S(2)}) copy-start(f32[2,16,32]{2,1,0:T(8,128)} %get-tuple-element.131) | copy-start | bytes 12292
  154.4 15.8 %copy-start.16 = (f32[2]{0:T(128)S(1)}, f32[2]{0:T(128)}, u32[]{:S(2)}) copy-start(f32[2]{0:T(128)} %copy-done.14) | copy-start | bytes 28
  155.5 1.6 collective-permute-start.10
  155.6 4.1 %collective-permute-start.11 = (f32[2,1,16,32]{3,2,1,0:T(8,128)S(1)}, f32[2,1,16,32]{3,2,1,0:T(8,128)S(1)}, u32[]{:S(2)}, u32[]{:S(2)}) collective-permute-start(f32[2,1,16,32]{3,2,1,0:T(8,128)S(1)} %get-tuple-element.130), channel_id=1, source_target_pairs={{0,4},{4,8},{8,12},{12,16},{16,20},{20,24},{24,28},{28,0},{1,5},{5... | collective-permute-start | bytes 12296 | tf_op jit(solution)/shard_map/ppermute | solution.py:18
  160.8 1.5 collective-permute-start.12
  160.8 4.1 %collective-permute-start.13 = (f32[2,1,16,32]{3,2,1,0:T(8,128)S(1)}, f32[2,1,16,32]{3,2,1,0:T(8,128)S(1)}, u32[]{:S(2)}, u32[]{:S(2)}) collective-permute-start(f32[2,1,16,32]{3,2,1,0:T(8,128)S(1)} %get-tuple-element.120), channel_id=1, source_target_pairs={{0,4},{4,8},{8,12},{12,16},{16,20},{20,24},{24,28},{28,0},{1,5},{5... | collective-permute-start | bytes 12296 | tf_op jit(solution)/shard_map/ppermute | solution.py:18
  166.0 1.5 collective-permute-start.14
  166.1 4.1 %collective-permute-start.15 = (f32[2,1,16,32]{3,2,1,0:T(8,128)S(1)}, f32[2,1,16,32]{3,2,1,0:T(8,128)S(1)}, u32[]{:S(2)}, u32[]{:S(2)}) collective-permute-start(f32[2,1,16,32]{3,2,1,0:T(8,128)S(1)} %get-tuple-element.110), channel_id=1, source_target_pairs={{0,4},{4,8},{8,12},{12,16},{16,20},{20,24},{24,28},{28,0},{1,5},{5... | collective-permute-start | bytes 12296 | tf_op jit(solution)/shard_map/ppermute | solution.py:18
  177.1 10.0 %copy-start.17 = (f32[2]{0:T(128)S(1)}, f32[2]{0:T(128)}, u32[]{:S(2)}) copy-start(f32[2]{0:T(128)} %copy-done.14) | copy-start | bytes 28
  177.3 1.7 collective-permute-start.16
  177.3 4.3 %collective-permute-start.17 = (f32[2,1,32,64]{3,2,1,0:T(8,128)S(1)}, f32[2,1,32,64]{3,2,1,0:T(8,128)S(1)}, u32[]{:S(2)}, u32[]{:S(2)}) collective-permute-start(f32[2,1,32,64]{3,2,1,0:T(8,128)S(1)} %get-tuple-element.78), channel_id=1, source_target_pairs={{0,4},{4,8},{8,12},{12,16},{16,20},{20,24},{24,28},{28,0},{1,5},{5... | collective-permute-start | bytes 49160 | tf_op jit(solution)/shard_map/ppermute | solution.py:18
  182.7 1.8 collective-permute-start.18
  182.9 4.2 %collective-permute-start.19 = (f32[2,1,32,64]{3,2,1,0:T(8,128)S(1)}, f32[2,1,32,64]{3,2,1,0:T(8,128)S(1)}, u32[]{:S(2)}, u32[]{:S(2)}) collective-permute-start(f32[2,1,32,64]{3,2,1,0:T(8,128)S(1)} %get-tuple-element.68), channel_id=1, source_target_pairs={{0,4},{4,8},{8,12},{12,16},{16,20},{20,24},{24,28},{28,0},{1,5},{5... | collective-permute-start | bytes 49160 | tf_op jit(solution)/shard_map/ppermute | solution.py:18
  192.1 3.8 %collective-permute-start.20 = (f32[2,1,64,128]{2,1,3,0:T(1,128)S(1)}, f32[2,1,64,128]{2,1,3,0:T(1,128)S(1)}, u32[]{:S(2)}, u32[]{:S(2)}) collective-permute-start(f32[2,1,64,128]{2,1,3,0:T(1,128)S(1)} %get-tuple-element.25), channel_id=1, source_target_pairs={{4,0},{8,4},{12,8},{16,12},{20,16},{24,20},{28,24},{0,28},{5,1},{9... | collective-permute-start | bytes 196616 | tf_op jit(solution)/shard_map/ppermute | solution.py:21
  192.2 5.3 %collective-permute-start.21 = (f32[2,1,64,128]{2,1,3,0:T(1,128)S(1)}, f32[2,1,64,128]{2,1,3,0:T(1,128)S(1)}, u32[]{:S(2)}, u32[]{:S(2)}) collective-permute-start(f32[2,1,64,128]{2,1,3,0:T(1,128)S(1)} %get-tuple-element.26), channel_id=1, source_target_pairs={{0,4},{4,8},{8,12},{12,16},{16,20},{20,24},{24,28},{28,0},{1,5},{5... | collective-permute-start | bytes 196616 | tf_op jit(solution)/shard_map/ppermute | solution.py:18
  192.8 4.7 %copy-start.2 = (f32[8,64,128]{1,0,2:T(8,128)S(1)}, f32[8,64,128]{1,0,2:T(8,128)}, u32[]{:S(2)}) copy-start(f32[8,64,128]{1,0,2:T(8,128)} %copy-done) | copy-start | bytes 786436
  192.8 4.7 %copy-start.5 = (f32[8,64,128]{1,0,2:T(8,128)S(1)}, f32[8,64,128]{1,0,2:T(8,128)}, u32[]{:S(2)}) copy-start(f32[8,64,128]{1,0,2:T(8,128)} %copy-done.3) | copy-start | bytes 786436
  199.1 4.2 %collective-permute-start.22 = (f32[2,1,64,128]{2,1,3,0:T(1,128)S(1)}, f32[2,1,64,128]{2,1,3,0:T(1,128)S(1)}, u32[]{:S(2)}, u32[]{:S(2)}) collective-permute-start(f32[2,1,64,128]{2,1,3,0:T(1,128)S(1)} %get-tuple-element.15), channel_id=1, source_target_pairs={{4,0},{8,4},{12,8},{16,12},{20,16},{24,20},{28,24},{0,28},{5,1},{9... | collective-permute-start | bytes 196616 | tf_op jit(solution)/shard_map/ppermute | solution.py:21
  200.6 5.3 %collective-permute-start.23 = (f32[2,1,64,128]{2,1,3,0:T(1,128)S(1)}, f32[2,1,64,128]{2,1,3,0:T(1,128)S(1)}, u32[]{:S(2)}, u32[]{:S(2)}) collective-permute-start(f32[2,1,64,128]{2,1,3,0:T(1,128)S(1)} %get-tuple-element.16), channel_id=1, source_target_pairs={{0,4},{4,8},{8,12},{12,16},{16,20},{20,24},{24,28},{28,0},{1,5},{5... | collective-permute-start | bytes 196616 | tf_op jit(solution)/shard_map/ppermute | solution.py:18
  208.2 9.2 %copy-start.6 = (f32[2,8,64,128]{2,1,3,0:T(8,128)S(1)}, f32[2,8,64,128]{2,1,3,0:T(8,128)}, u32[]{:S(2)}) copy-start(f32[2,8,64,128]{2,1,3,0:T(8,128)} %fusion.13) | copy-start | bytes 1572868
  210.7 20.0 %copy-start.7 = (f32[8,8,64,128]{3,2,1,0:T(8,128)S(1)}, f32[8,8,64,128]{3,2,1,0:T(8,128)}, u32[]{:S(2)}) copy-start(f32[8,8,64,128]{3,2,1,0:T(8,128)} %all-gather.2.cloned.1.call-done) | copy-start | bytes 6291460
Sparse Core Ops, SparseCore 0:
  11.0 47.1 all-gather.1
where the time goes:
time: 244 us; the launch traced here: 242 us
  local copies, waits for them, and re-layouts  101 us (41%)
  other arithmetic  45.7 us (19%)
  waiting for transfers between devices  45.6 us (19%)
  between operations  14 us (6%)
  starting transfers between devices  13.1 us (5%)
  blocking collectives  12.1 us (5%)
  matrix products  10.9 us (4%)
    reshape x2, local copies, waits for them, and re-layouts, coarsen(): field_values.reshape(lead, sx // 2, 2, sy // 2, 2, sz // 2, 2)  42.1 us
    ppermute x12, waiting for transfers between devices, with_halo(): lax.ppermute(lax.slice_in_dim(block, block.shape[dim] - width, None, axis...  27.4 us
    reduce_sum x4, other arithmetic, coarsen(): field_values.reshape(lead, sx // 2, 2, sy // 2, 2, sz // 2, 2)  24.3 us
    ppermute x12, waiting for transfers between devices, with_halo(): lax.ppermute(lax.slice_in_dim(block, 0, width, axis=dim), axis, backward)  18.2 us
    another operation x1, local copies, waits for them, and re-layouts, coarsen(): field_values.reshape(lead, sx // 2, 2, sy // 2, 2, sz // 2, 2)  18.1 us
    psum x1, blocking collectives, on_device(): intersection = lax.psum(partial_intersection, 'dom') / cells_total  12.1 us
    ppermute x12, starting transfers between devices, with_halo(): lax.ppermute(lax.slice_in_dim(block, 0, width, axis=dim), axis, backward)  9.35 us
    unnamed x51, local copies, waits for them, and re-layouts  8.67 us
  transfers between devices with their start and end apart: 25, of which 22 were waited for; matrix products, arithmetic and copies ran while one was open for 59% of the time, Pallas kernels for 0%

commit v1 on v0

--- a/solution.py
+++ b/solution.py
@@ -112,7 +112,7 @@
     partial_intersection = jnp.einsum(
         "jc,ic->ji", flat_orbit, flat_update, precision=lax.Precision.HIGHEST
     )
-    intersection = lax.psum(partial_intersection, "dom") / cells_total
+    intersection = jnp.sum(lax.all_gather(partial_intersection, "dom"), axis=0) / cells_total
     corrected = flat_update - jnp.einsum(
         "ji,jc->ic", intersection, flat_orbit, precision=lax.Precision.HIGHEST
     )

time: 244 us -> 237 us (0.971)
  blocking collectives: 12.1 us -> 7.94 us
    psum x1 -> x0, blocking collectives: 12.1 us -> none  [on_device(): intersection = lax.psum(partial_intersection, 'dom') / cells_total]
    all_gather x0 -> x1, blocking collectives: none -> 7.94 us  [on_device(): lax.all_gather(partial_intersection, 'dom')]
  transfers between devices with their start and end apart: 25 -> 25, of which waited for: 22 -> 22; matrix products, arithmetic and copies ran while one was open for 59% -> 61% of each run, Pallas kernels for 0% -> 0%
where the time goes in v1:
time: 237 us; the launch traced here: 236 us
  local copies, waits for them, and re-layouts  99.5 us (42%)
  waiting for transfers between devices  45.7 us (19%)
  other arithmetic  45.7 us (19%)
  between operations  14 us (6%)
  starting transfers between devices  13.1 us (6%)
  matrix products  9.7 us (4%)
  blocking collectives  7.94 us (3%)
    reshape x2, local copies, waits for them, and re-layouts, coarsen(): field_values.reshape(lead, sx // 2, 2, sy // 2, 2, sz // 2, 2)  42.1 us
    ppermute x12, waiting for transfers between devices, with_halo(): lax.ppermute(lax.slice_in_dim(block, block.shape[dim] - width, None, axis...  27.4 us
    reduce_sum x4, other arithmetic, coarsen(): field_values.reshape(lead, sx // 2, 2, sy // 2, 2, sz // 2, 2)  24.3 us
    ppermute x12, waiting for transfers between devices, with_halo(): lax.ppermute(lax.slice_in_dim(block, 0, width, axis=dim), axis, backward)  18.2 us
    another operation x1, local copies, waits for them, and re-layouts, coarsen(): field_values.reshape(lead, sx // 2, 2, sy // 2, 2, sz // 2, 2)  18.1 us
    ppermute x12, starting transfers between devices, with_halo(): lax.ppermute(lax.slice_in_dim(block, 0, width, axis=dim), axis, backward)  9.35 us
    unnamed x51, local copies, waits for them, and re-layouts  8.67 us
    all_gather x1, blocking collectives, on_device(): lax.all_gather(partial_intersection, 'dom')  7.94 us
  transfers between devices with their start and end apart: 25, of which 22 were waited for; matrix products, arithmetic and copies ran while one was open for 61% of the time, Pallas kernels for 0%

profile of v1, /device:TPU:0, one launch (start us, length us, event | category | flops | bytes accessed | tf_op | source)
XLA Modules:
  0.0 235.7 jit_solution(14274011410103325921)
XLA Ops:
  6.5 0.9 fusion.140
  7.4 3.4 %collective-permute-start = (f32[2,1,64,128]{3,2,1,0:T(8,128)S(1)}, f32[2,1,64,128]{3,2,1,0:T(8,128)S(1)}, u32[]{:S(2)}, u32[]{:S(2)}) collective-permute-start(f32[2,1,64,128]{3,2,1,0:T(8,128)S(1)} %get-tuple-element.56), channel_id=1, source_target_pairs={{4,0},{8,4},{12,8},{16,12},{20,16},{24,20},{28,24},{0,28},{5,1},{9... | collective-permute-start | bytes 196616 | tf_op jit(solution)/shard_map/ppermute | solution.py:21
  10.9 1.4 copy.135
  12.3 1.6 fusion.137
  13.9 1.5 fusion.138
  16.4 1.3 copy.115
  17.7 18.1 %reshape_broadcast_in_dim.3 = f32[4,2,32,2,64,2]{5,4,3,2,1,0:T(8,128)} reshape(f32[8,64,128]{2,1,0:T(8,128)S(1)} %copy-done.9) | data formatting | bytes 524288 | tf_op jit(solution)/shard_map/reshape;broadcast_in_dim | solution.py:53
  36.0 1.4 copy.120
  37.4 1.4 copy.122
  38.8 1.0 copy.114
  39.8 7.1 %reduce_sum.56 = f32[4,32,64]{2,1,0:T(8,128)S(1)} reduce(f32[4,2,32,2,64,2]{5,4,3,2,1,0:T(8,128)} %reshape_broadcast_in_dim.3, f32[]{:T(128)} %constant.14.clone.1), dimensions={1,3,5}, to_apply=%region_2.0 | reduce | flops 57344 | bytes 294916 | tf_op jit(solution)/shard_map/reduce_sum | solution.py:53
  46.9 3.5 %div.73 = f32[2,2,16,2,32,2]{5,4,3,2,1,0:T(8,128)} reshape(f32[4,32,64]{2,1,0:T(8,128)S(1)} %get-tuple-element.99) | data formatting | bytes 65536 | tf_op jit(solution)/shard_map/div | solution.py:53
  50.4 1.8 reduce_sum.58
  53.0 1.8 pad_maximum_fusion.8
  54.8 2.3 copy.140
  57.1 1.4 copy.141
  58.6 4.9 %add_divide_fusion.3 = (f32[2,8,64,128]{2,1,3,0:T(8,128)S(1)}, f32[2,8,64,128]{2,1,3,0:T(8,128)S(1)}) fusion(f32[8,64,128]{1,0,2:T(8,128)S(1)} %copy.129, f32[2]{0:T(128)S(1)} %fusion.112, f32[2,8,64,128]{2,1,3,0:T(8,128)S(1)} %copy.135, f32[8,64,128]{1,0,2:T(8,128)S(1)} %copy.127, f32[2,8,64,127]{2,1,3,0:T(8,128)} %get-tuple-element.50, ...), kind=kLoop, calls=%fused_computation.9 | loop fusion | flops 2752512 | bytes 6029320 | tf_op jit(solution)/shard_map/div | solution.py:87
  64.4 2.7 %collective-permute-start.2 = (f32[2,1,64,128]{2,1,3,0:T(1,128)S(1)}, f32[2,1,64,128]{2,1,3,0:T(1,128)S(1)}, u32[]{:S(2)}, u32[]{:S(2)}) collective-permute-start(f32[2,1,64,128]{2,1,3,0:T(1,128)S(1)} %get-tuple-element.45), channel_id=1, source_target_pairs={{4,0},{8,4},{12,8},{16,12},{20,16},{24,20},{28,24},{0,28},{5,1},{9... | collective-permute-start | bytes 196616 | tf_op jit(solution)/shard_map/ppermute | solution.py:21
  67.1 2.5 %collective-permute-done.2 = f32[2,1,64,128]{2,1,3,0:T(1,128)S(1)} collective-permute-done((f32[2,1,64,128]{2,1,3,0:T(1,128)S(1)}, f32[2,1,64,128]{2,1,3,0:T(1,128)S(1)}, u32[]{:S(2)}, u32[]{:S(2)}) %collective-permute-start.2) | collective-permute-done | bytes 65568 | tf_op jit(solution)/shard_map/ppermute | solution.py:21
  69.7 2.8 %collective-permute-done.3 = f32[2,1,64,128]{2,1,3,0:T(1,128)S(1)} collective-permute-done((f32[2,1,64,128]{2,1,3,0:T(1,128)S(1)}, f32[2,1,64,128]{2,1,3,0:T(1,128)S(1)}, u32[]{:S(2)}, u32[]{:S(2)}) %collective-permute-start.3) | collective-permute-done | bytes 65568 | tf_op jit(solution)/shard_map/ppermute | solution.py:18
  72.4 1.4 fusion.10
  75.4 3.2 %collective-permute-done.4 = f32[2,1,64,128]{2,1,3,0:T(1,128)S(1)} collective-permute-done((f32[2,1,64,128]{2,1,3,0:T(1,128)S(1)}, f32[2,1,64,128]{2,1,3,0:T(1,128)S(1)}, u32[]{:S(2)}, u32[]{:S(2)}) %collective-permute-start.4) | collective-permute-done | bytes 65568 | tf_op jit(solution)/shard_map/ppermute | solution.py:21
  78.6 1.8 collective-permute-done.5
  80.4 2.2 fusion.20
  82.7 2.3 copy.130
  85.0 35.6 %reshape.71 = f32[2,4,2,32,2,64,2]{6,5,4,3,2,1,0:T(8,128)} reshape(f32[2,8,64,128]{3,2,1,0:T(8,128)} %copy.130) | data formatting | bytes 1048576 | tf_op jit(solution)/shard_map/reshape | solution.py:53
  120.6 12.2 %reduce_sum.55 = f32[2,4,32,64]{3,2,1,0:T(8,128)S(1)} reduce(f32[2,4,2,32,2,64,2]{6,5,4,3,2,1,0:T(8,128)} %reshape.71, f32[]{:T(128)} %constant.14.clone.1), dimensions={2,4,6}, to_apply=%region_1.0 | reduce | flops 114688 | bytes 589828 | tf_op jit(solution)/shard_map/reduce_sum | solution.py:53
  133.2 1.0 collective-permute-start.6
  134.2 1.6 collective-permute-done.6
  135.8 2.6 %collective-permute-done.7 = f32[2,1,32,64]{3,2,1,0:T(8,128)S(1)} collective-permute-done((f32[2,1,32,64]{3,2,1,0:T(8,128)S(1)}, f32[2,1,32,64]{3,2,1,0:T(8,128)S(1)}, u32[]{:S(2)}, u32[]{:S(2)}) %collective-permute-start.7) | collective-permute-done | bytes 16416 | tf_op jit(solution)/shard_map/ppermute | solution.py:18
  140.1 1.1 collective-permute-done.8
  141.2 2.7 %collective-permute-done.9 = f32[2,1,32,64]{3,2,1,0:T(8,128)S(1)} collective-permute-done((f32[2,1,32,64]{3,2,1,0:T(8,128)S(1)}, f32[2,1,32,64]{3,2,1,0:T(8,128)S(1)}, u32[]{:S(2)}, u32[]{:S(2)}) %collective-permute-start.9) | collective-permute-done | bytes 16416 | tf_op jit(solution)/shard_map/ppermute | solution.py:18
  144.7 6.5 %reshape.72 = f32[2,2,2,16,2,32,2]{6,5,4,3,2,1,0:T(8,128)} reshape(f32[2,4,32,64]{3,2,1,0:T(8,128)} %fusion.58) | data formatting | bytes 131072 | tf_op jit(solution)/shard_map/reshape | solution.py:53
  151.2 3.2 %reduce_sum.57 = f32[2,2,16,32]{3,2,1,0:T(8,128)} reduce(f32[2,2,2,16,2,32,2]{6,5,4,3,2,1,0:T(8,128)} %reshape.72, f32[]{:T(128)} %constant.14.clone.1), dimensions={2,4,6}, to_apply=%region_3.4 | reduce | flops 14336 | bytes 73732 | tf_op jit(solution)/shard_map/reduce_sum | solution.py:53
  154.4 0.9 add_divide_fusion.11
  156.0 1.0 collective-permute-done.10
  157.1 2.6 %collective-permute-done.11 = f32[2,1,16,32]{3,2,1,0:T(8,128)S(1)} collective-permute-done((f32[2,1,16,32]{3,2,1,0:T(8,128)S(1)}, f32[2,1,16,32]{3,2,1,0:T(8,128)S(1)}, u32[]{:S(2)}, u32[]{:S(2)}) %collective-permute-start.11) | collective-permute-done | bytes 4128 | tf_op jit(solution)/shard_map/ppermute | solution.py:18
  159.7 0.9 fusion.88
  161.3 0.9 collective-permute-done.12
  162.3 2.7 %collective-permute-done.13 = f32[2,1,16,32]{3,2,1,0:T(8,128)S(1)} collective-permute-done((f32[2,1,16,32]{3,2,1,0:T(8,128)S(1)}, f32[2,1,16,32]{3,2,1,0:T(8,128)S(1)}, u32[]{:S(2)}, u32[]{:S(2)}) %collective-permute-start.13) | collective-permute-done | bytes 4128 | tf_op jit(solution)/shard_map/ppermute | solution.py:18
  165.0 0.9 fusion.92
  166.6 0.9 collective-permute-done.14
  167.5 2.7 %collective-permute-done.15 = f32[2,1,16,32]{3,2,1,0:T(8,128)S(1)} collective-permute-done((f32[2,1,16,32]{3,2,1,0:T(8,128)S(1)}, f32[2,1,16,32]{3,2,1,0:T(8,128)S(1)}, u32[]{:S(2)}, u32[]{:S(2)}) %collective-permute-start.15) | collective-permute-done | bytes 4128 | tf_op jit(solution)/shard_map/ppermute | solution.py:18
  171.0 1.6 copy.131
  172.7 1.7 broadcast_in_dim.26
  174.4 1.7 copy.132
  176.1 0.9 add.550
  177.8 1.1 collective-permute-done.16
  178.9 2.7 %collective-permute-done.17 = f32[2,1,32,64]{3,2,1,0:T(8,128)S(1)} collective-permute-done((f32[2,1,32,64]{3,2,1,0:T(8,128)S(1)}, f32[2,1,32,64]{3,2,1,0:T(8,128)S(1)}, u32[]{:S(2)}, u32[]{:S(2)}) %collective-permute-start.17) | collective-permute-done | bytes 16416 | tf_op jit(solution)/shard_map/ppermute | solution.py:18
  183.3 1.2 collective-permute-done.18
  184.5 2.6 %collective-permute-done.19 = f32[2,1,32,64]{3,2,1,0:T(8,128)S(1)} collective-permute-done((f32[2,1,32,64]{3,2,1,0:T(8,128)S(1)}, f32[2,1,32,64]{3,2,1,0:T(8,128)S(1)}, u32[]{:S(2)}, u32[]{:S(2)}) %collective-permute-start.19) | collective-permute-done | bytes 16416 | tf_op jit(solution)/shard_map/ppermute | solution.py:18
  188.3 2.1 copy.134
  190.4 1.1 broadcast_in_dim.29
  193.2 2.7 %collective-permute-done.20 = f32[2,1,64,128]{2,1,3,0:T(1,128)S(1)} collective-permute-done((f32[2,1,64,128]{2,1,3,0:T(1,128)S(1)}, f32[2,1,64,128]{2,1,3,0:T(1,128)S(1)}, u32[]{:S(2)}, u32[]{:S(2)}) %collective-permute-start.20) | collective-permute-done | bytes 65568 | tf_op jit(solution)/shard_map/ppermute | solution.py:21
  195.9 1.6 collective-permute-done.21
  197.5 1.4 fusion.11
  199.1 1.4 collective-permute-start.22
  201.4 2.0 collective-permute-done.22
  203.4 2.5 %collective-permute-done.23 = f32[2,1,64,128]{2,1,3,0:T(1,128)S(1)} collective-permute-done((f32[2,1,64,128]{2,1,3,0:T(1,128)S(1)}, f32[2,1,64,128]{2,1,3,0:T(1,128)S(1)}, u32[]{:S(2)}, u32[]{:S(2)}) %collective-permute-start.23) | collective-permute-done | bytes 65568 | tf_op jit(solution)/shard_map/ppermute | solution.py:18
  205.9 2.4 %fusion.13 = f32[2,8,64,128]{2,1,3,0:T(8,128)} fusion(f32[2,8,64,128]{2,1,3,0:T(8,128)S(1)} %copy.135, f32[2,8,64,128]{2,1,3,0:T(8,128)S(1)} %fusion.11, f32[2,8,64,128]{2,1,3,0:T(8,128)S(1)} %get-tuple-element.6, f32[2,1,64,128]{2,1,3,0:T(1,128)S(1)} %collective-permute-done.23, f32[2,1,64,128]{2,1,3,0:T(1,128)S(1)} %collective-permute-done.22, ...), kind=kLoop, calls=%fused_computation.19 | loop fusion | flops 3014656 | bytes 4849672 | tf_op jit(solution)/shard_map/add | solution.py:107
  208.2 1.7 copy.137
  210.3 6.6 %fusion.7 = f32[1,8,2]{1,2,0:T(2,128)S(1)} fusion(f32[2,8,64,128]{3,0,2,1:T(2,128)S(1)} %copy.137, f32[8,8,64,128]{3,2,1,0:T(8,128)} %all-gather.4.cloned.1.call-done), kind=kOutput, calls=%fused_computation.15 | convolution fusion | flops 12582912 | bytes 2621504 | tf_op jit(solution)/shard_map/jc,ic->ji/dot_general | solution.py:112
  216.9 7.9 %all-gather.1 = f32[8,8,2]{1,2,0:T(2,128)S(1)} all-gather(f32[1,8,2]{1,2,0:T(2,128)S(1)} %fusion.7), channel_id=2, replica_groups=mesh['dom'=8,'orb'=4] {'dom'}, dimensions={0}, use_global_device_ids=true | all-gather | bytes 576 | tf_op jit(solution)/shard_map/all_gather | solution.py:115
  224.9 3.1 %fusion.4 = f32[1,2,512,128]{3,1,2,0:T(2,128)S(1)} fusion(f32[1,8,512,128]{3,2,1,0:T(8,128)S(1)} %bitcast.34, f32[1,2,512,128]{3,2,1,0:T(8,128)S(1)} %bitcast.36, f32[8,2]{0,1:T(2,128)S(1)} %reduce_sum.59), kind=kOutput, calls=%fused_computation.14 | convolution fusion | flops 12714000 | bytes 3145792 | tf_op jit(solution)/shard_map/ji,jc->ic/dot_general | solution.py:116
  (147 shorter events, 17.7 us)
Async XLA Ops:
  6.5 203.8 %all-gather.4.cloned.1.call-start = ((), (), s32[]{:S(2)}) async-start(), calls=%async_computation | async-start | bytes 2621440 | tf_op jit(solution)/shard_map/all_gather | solution.py:109
  7.4 45.6 %collective-permute-start = (f32[2,1,64,128]{3,2,1,0:T(8,128)S(1)}, f32[2,1,64,128]{3,2,1,0:T(8,128)S(1)}, u32[]{:S(2)}, u32[]{:S(2)}) collective-permute-start(f32[2,1,64,128]{3,2,1,0:T(8,128)S(1)} %get-tuple-element.56), channel_id=1, source_target_pairs={{4,0},{8,4},{12,8},{16,12},{20,16},{24,20},{28,24},{0,28},{5,1},{9... | collective-permute-start | bytes 196616 | tf_op jit(solution)/shard_map/ppermute | solution.py:21
  10.8 42.2 %collective-permute-start.1 = (f32[2,1,64,128]{3,2,1,0:T(8,128)S(1)}, f32[2,1,64,128]{3,2,1,0:T(8,128)}, u32[]{:S(2)}, u32[]{:S(2)}) collective-permute-start(f32[2,1,64,128]{3,2,1,0:T(8,128)S(1)} %get-tuple-element.55), channel_id=1, source_target_pairs={{0,4},{4,8},{8,12},{12,16},{16,20},{20,24},{24,28},{28,0},{1,5},{5... | collective-permute-start | bytes 196616 | tf_op jit(solution)/shard_map/ppermute | solution.py:18
  13.9 2.1 copy-start.9
  13.9 2.4 %copy-start.8 = (f32[2,8,64,128]{3,2,1,0:T(8,128)S(1)}, f32[2,8,64,128]{3,2,1,0:T(8,128)}, u32[]{:S(2)}) copy-start(f32[2,8,64,128]{3,2,1,0:T(8,128)} %param.7) | copy-start | bytes 1572868
  13.9 2.4 %copy-start.10 = (f32[2,8,64,128]{3,2,1,0:T(8,128)S(1)}, f32[2,8,64,128]{3,2,1,0:T(8,128)}, u32[]{:S(2)}) copy-start(f32[2,8,64,128]{3,2,1,0:T(8,128)} %param.6) | copy-start | bytes 1572868
  16.3 42.2 %copy-start = (f32[8,64,128]{1,0,2:T(8,128)}, f32[8,64,128]{1,0,2:T(8,128)S(1)}, u32[]{:S(2)}) copy-start(f32[8,64,128]{1,0,2:T(8,128)S(1)} %copy.127) | copy-start | bytes 786436
  35.7 3.0 %copy-start.12 = (f32[8,64,128]{2,1,0:T(8,128)S(1)}, f32[8,64,128]{2,1,0:T(8,128)}, u32[]{:S(2)}) copy-start(f32[8,64,128]{2,1,0:T(8,128)} %param.9) | copy-start | bytes 786436
  36.0 22.5 %copy-start.3 = (f32[8,64,128]{1,0,2:T(8,128)}, f32[8,64,128]{1,0,2:T(8,128)S(1)}, u32[]{:S(2)}) copy-start(f32[8,64,128]{1,0,2:T(8,128)S(1)} %copy.129) | copy-start | bytes 786436
  46.9 5.9 %copy-start.20 = (f32[8]{0:T(128)S(1)}, f32[8]{0:T(128)}, u32[]{:S(2)}) copy-start(f32[8]{0:T(128)} %param.10) | copy-start | bytes 100
  46.9 5.9 %copy-start.21 = (s32[2]{0:T(128)S(1)}, s32[2]{0:T(128)}, u32[]{:S(2)}) copy-start(s32[2]{0:T(128)} %param.11) | copy-start | bytes 28
  53.0 79.9 %copy-start.14 = (f32[2]{0:T(128)}, f32[2]{0:T(128)S(1)}, u32[]{:S(2)}) copy-start(f32[2]{0:T(128)S(1)} %fusion.112) | copy-start | bytes 28
  53.0 5.6 %copy-start.18 = (f32[2,8,64,1]{2,1,3,0:T(8,128)S(1)}, f32[2,8,64,1]{2,1,3,0:T(8,128)}, u32[]{:S(2)}) copy-start(f32[2,8,64,1]{2,1,3,0:T(8,128)} %get-tuple-element.51) | copy-start | bytes 12292
  53.0 5.6 %copy-start.19 = (f32[2,8,64,1]{2,1,3,0:T(8,128)S(1)}, f32[2,8,64,1]{2,1,3,0:T(8,128)}, u32[]{:S(2)}) copy-start(f32[2,8,64,1]{2,1,3,0:T(8,128)} %get-tuple-element.52) | copy-start | bytes 12292
  64.1 8.3 %copy-start.1 = (f32[8,64,128]{1,0,2:T(8,128)S(1)}, f32[8,64,128]{1,0,2:T(8,128)}, u32[]{:S(2)}) copy-start(f32[8,64,128]{1,0,2:T(8,128)} %copy-done) | copy-start | bytes 786436
  64.1 8.3 %copy-start.4 = (f32[8,64,128]{1,0,2:T(8,128)S(1)}, f32[8,64,128]{1,0,2:T(8,128)}, u32[]{:S(2)}) copy-start(f32[8,64,128]{1,0,2:T(8,128)} %copy-done.3) | copy-start | bytes 786436
  64.4 5.2 %collective-permute-start.2 = (f32[2,1,64,128]{2,1,3,0:T(1,128)S(1)}, f32[2,1,64,128]{2,1,3,0:T(1,128)S(1)}, u32[]{:S(2)}, u32[]{:S(2)}) collective-permute-start(f32[2,1,64,128]{2,1,3,0:T(1,128)S(1)} %get-tuple-element.45), channel_id=1, source_target_pairs={{4,0},{8,4},{12,8},{16,12},{20,16},{24,20},{28,24},{0,28},{5,1},{9... | collective-permute-start | bytes 196616 | tf_op jit(solution)/shard_map/ppermute | solution.py:21
  67.1 5.3 %collective-permute-start.3 = (f32[2,1,64,128]{2,1,3,0:T(1,128)S(1)}, f32[2,1,64,128]{2,1,3,0:T(1,128)S(1)}, u32[]{:S(2)}, u32[]{:S(2)}) collective-permute-start(f32[2,1,64,128]{2,1,3,0:T(1,128)S(1)} %get-tuple-element.46), channel_id=1, source_target_pairs={{0,4},{4,8},{8,12},{12,16},{16,20},{20,24},{24,28},{28,0},{1,5},{5... | collective-permute-start | bytes 196616 | tf_op jit(solution)/shard_map/ppermute | solution.py:18
  74.8 3.8 %collective-permute-start.4 = (f32[2,1,64,128]{2,1,3,0:T(1,128)S(1)}, f32[2,1,64,128]{2,1,3,0:T(1,128)S(1)}, u32[]{:S(2)}, u32[]{:S(2)}) collective-permute-start(f32[2,1,64,128]{2,1,3,0:T(1,128)S(1)} %get-tuple-element.35), channel_id=1, source_target_pairs={{4,0},{8,4},{12,8},{16,12},{20,16},{24,20},{28,24},{0,28},{5,1},{9... | collective-permute-start | bytes 196616 | tf_op jit(solution)/shard_map/ppermute | solution.py:21
  74.9 5.5 %collective-permute-start.5 = (f32[2,1,64,128]{2,1,3,0:T(1,128)S(1)}, f32[2,1,64,128]{2,1,3,0:T(1,128)S(1)}, u32[]{:S(2)}, u32[]{:S(2)}) collective-permute-start(f32[2,1,64,128]{2,1,3,0:T(1,128)S(1)} %get-tuple-element.36), channel_id=1, source_target_pairs={{0,4},{4,8},{8,12},{12,16},{16,20},{20,24},{24,28},{28,0},{1,5},{5... | collective-permute-start | bytes 196616 | tf_op jit(solution)/shard_map/ppermute | solution.py:18
  133.0 10.8 %copy-start.15 = (f32[2]{0:T(128)S(1)}, f32[2]{0:T(128)}, u32[]{:S(2)}) copy-start(f32[2]{0:T(128)} %copy-done.14) | copy-start | bytes 28
  133.2 2.6 %collective-permute-start.6 = (f32[2,1,32,64]{3,2,1,0:T(8,128)S(1)}, f32[2,1,32,64]{3,2,1,0:T(8,128)S(1)}, u32[]{:S(2)}, u32[]{:S(2)}) collective-permute-start(f32[2,1,32,64]{3,2,1,0:T(8,128)S(1)} %get-tuple-element.97), channel_id=1, source_target_pairs={{4,0},{8,4},{12,8},{16,12},{20,16},{24,20},{28,24},{0,28},{5,1},{9... | collective-permute-start | bytes 49160 | tf_op jit(solution)/shard_map/ppermute | solution.py:21
  134.2 4.2 %collective-permute-start.7 = (f32[2,1,32,64]{3,2,1,0:T(8,128)S(1)}, f32[2,1,32,64]{3,2,1,0:T(8,128)S(1)}, u32[]{:S(2)}, u32[]{:S(2)}) collective-permute-start(f32[2,1,32,64]{3,2,1,0:T(8,128)S(1)} %get-tuple-element.98), channel_id=1, source_target_pairs={{0,4},{4,8},{8,12},{12,16},{16,20},{20,24},{24,28},{28,0},{1,5},{5... | collective-permute-start | bytes 49160 | tf_op jit(solution)/shard_map/ppermute | solution.py:18
  139.5 1.7 collective-permute-start.8
  139.6 4.3 %collective-permute-start.9 = (f32[2,1,32,64]{3,2,1,0:T(8,128)S(1)}, f32[2,1,32,64]{3,2,1,0:T(8,128)S(1)}, u32[]{:S(2)}, u32[]{:S(2)}) collective-permute-start(f32[2,1,32,64]{3,2,1,0:T(8,128)S(1)} %get-tuple-element.88), channel_id=1, source_target_pairs={{0,4},{4,8},{8,12},{12,16},{16,20},{20,24},{24,28},{28,0},{1,5},{5... | collective-permute-start | bytes 49160 | tf_op jit(solution)/shard_map/ppermute | solution.py:18
  154.4 15.8 %copy-start.11 = (f32[2,2,16,32]{3,2,1,0:T(8,128)S(1)}, f32[2,2,16,32]{3,2,1,0:T(8,128)}, u32[]{:S(2)}) copy-start(f32[2,2,16,32]{3,2,1,0:T(8,128)} %reduce_sum.57) | copy-start | bytes 24580
  154.4 15.8 %copy-start.13 = (f32[2,16,32]{2,1,0:T(8,128)S(1)}, f32[2,16,32]{2,1,0:T(8,128)}, u32[]{:S(2)}) copy-start(f32[2,16,32]{2,1,0:T(8,128)} %get-tuple-element.131) | copy-start | bytes 12292
  154.4 15.8 %copy-start.16 = (f32[2]{0:T(128)S(1)}, f32[2]{0:T(128)}, u32[]{:S(2)}) copy-start(f32[2]{0:T(128)} %copy-done.14) | copy-start | bytes 28
  155.5 1.6 collective-permute-start.10
  155.6 4.1 %collective-permute-start.11 = (f32[2,1,16,32]{3,2,1,0:T(8,128)S(1)}, f32[2,1,16,32]{3,2,1,0:T(8,128)S(1)}, u32[]{:S(2)}, u32[]{:S(2)}) collective-permute-start(f32[2,1,16,32]{3,2,1,0:T(8,128)S(1)} %get-tuple-element.130), channel_id=1, source_target_pairs={{0,4},{4,8},{8,12},{12,16},{16,20},{20,24},{24,28},{28,0},{1,5},{5... | collective-permute-start | bytes 12296 | tf_op jit(solution)/shard_map/ppermute | solution.py:18
  160.8 1.5 collective-permute-start.12
  160.8 4.1 %collective-permute-start.13 = (f32[2,1,16,32]{3,2,1,0:T(8,128)S(1)}, f32[2,1,16,32]{3,2,1,0:T(8,128)S(1)}, u32[]{:S(2)}, u32[]{:S(2)}) collective-permute-start(f32[2,1,16,32]{3,2,1,0:T(8,128)S(1)} %get-tuple-element.120), channel_id=1, source_target_pairs={{0,4},{4,8},{8,12},{12,16},{16,20},{20,24},{24,28},{28,0},{1,5},{5... | collective-permute-start | bytes 12296 | tf_op jit(solution)/shard_map/ppermute | solution.py:18
  166.0 1.5 collective-permute-start.14
  166.1 4.1 %collective-permute-start.15 = (f32[2,1,16,32]{3,2,1,0:T(8,128)S(1)}, f32[2,1,16,32]{3,2,1,0:T(8,128)S(1)}, u32[]{:S(2)}, u32[]{:S(2)}) collective-permute-start(f32[2,1,16,32]{3,2,1,0:T(8,128)S(1)} %get-tuple-element.110), channel_id=1, source_target_pairs={{0,4},{4,8},{8,12},{12,16},{16,20},{20,24},{24,28},{28,0},{1,5},{5... | collective-permute-start | bytes 12296 | tf_op jit(solution)/shard_map/ppermute | solution.py:18
  177.1 10.0 %copy-start.17 = (f32[2]{0:T(128)S(1)}, f32[2]{0:T(128)}, u32[]{:S(2)}) copy-start(f32[2]{0:T(128)} %copy-done.14) | copy-start | bytes 28
  177.3 1.7 collective-permute-start.16
  177.3 4.3 %collective-permute-start.17 = (f32[2,1,32,64]{3,2,1,0:T(8,128)S(1)}, f32[2,1,32,64]{3,2,1,0:T(8,128)S(1)}, u32[]{:S(2)}, u32[]{:S(2)}) collective-permute-start(f32[2,1,32,64]{3,2,1,0:T(8,128)S(1)} %get-tuple-element.78), channel_id=1, source_target_pairs={{0,4},{4,8},{8,12},{12,16},{16,20},{20,24},{24,28},{28,0},{1,5},{5... | collective-permute-start | bytes 49160 | tf_op jit(solution)/shard_map/ppermute | solution.py:18
  182.7 1.8 collective-permute-start.18
  182.9 4.2 %collective-permute-start.19 = (f32[2,1,32,64]{3,2,1,0:T(8,128)S(1)}, f32[2,1,32,64]{3,2,1,0:T(8,128)S(1)}, u32[]{:S(2)}, u32[]{:S(2)}) collective-permute-start(f32[2,1,32,64]{3,2,1,0:T(8,128)S(1)} %get-tuple-element.68), channel_id=1, source_target_pairs={{0,4},{4,8},{8,12},{12,16},{16,20},{20,24},{24,28},{28,0},{1,5},{5... | collective-permute-start | bytes 49160 | tf_op jit(solution)/shard_map/ppermute | solution.py:18
  192.1 3.8 %collective-permute-start.20 = (f32[2,1,64,128]{2,1,3,0:T(1,128)S(1)}, f32[2,1,64,128]{2,1,3,0:T(1,128)S(1)}, u32[]{:S(2)}, u32[]{:S(2)}) collective-permute-start(f32[2,1,64,128]{2,1,3,0:T(1,128)S(1)} %get-tuple-element.25), channel_id=1, source_target_pairs={{4,0},{8,4},{12,8},{16,12},{20,16},{24,20},{28,24},{0,28},{5,1},{9... | collective-permute-start | bytes 196616 | tf_op jit(solution)/shard_map/ppermute | solution.py:21
  192.2 5.3 %collective-permute-start.21 = (f32[2,1,64,128]{2,1,3,0:T(1,128)S(1)}, f32[2,1,64,128]{2,1,3,0:T(1,128)S(1)}, u32[]{:S(2)}, u32[]{:S(2)}) collective-permute-start(f32[2,1,64,128]{2,1,3,0:T(1,128)S(1)} %get-tuple-element.26), channel_id=1, source_target_pairs={{0,4},{4,8},{8,12},{12,16},{16,20},{20,24},{24,28},{28,0},{1,5},{5... | collective-permute-start | bytes 196616 | tf_op jit(solution)/shard_map/ppermute | solution.py:18
  192.8 4.7 %copy-start.2 = (f32[8,64,128]{1,0,2:T(8,128)S(1)}, f32[8,64,128]{1,0,2:T(8,128)}, u32[]{:S(2)}) copy-start(f32[8,64,128]{1,0,2:T(8,128)} %copy-done) | copy-start | bytes 786436
  192.8 4.7 %copy-start.5 = (f32[8,64,128]{1,0,2:T(8,128)S(1)}, f32[8,64,128]{1,0,2:T(8,128)}, u32[]{:S(2)}) copy-start(f32[8,64,128]{1,0,2:T(8,128)} %copy-done.3) | copy-start | bytes 786436
  199.1 4.2 %collective-permute-start.22 = (f32[2,1,64,128]{2,1,3,0:T(1,128)S(1)}, f32[2,1,64,128]{2,1,3,0:T(1,128)S(1)}, u32[]{:S(2)}, u32[]{:S(2)}) collective-permute-start(f32[2,1,64,128]{2,1,3,0:T(1,128)S(1)} %get-tuple-element.15), channel_id=1, source_target_pairs={{4,0},{8,4},{12,8},{16,12},{20,16},{24,20},{28,24},{0,28},{5,1},{9... | collective-permute-start | bytes 196616 | tf_op jit(solution)/shard_map/ppermute | solution.py:21
  200.6 5.3 %collective-permute-start.23 = (f32[2,1,64,128]{2,1,3,0:T(1,128)S(1)}, f32[2,1,64,128]{2,1,3,0:T(1,128)S(1)}, u32[]{:S(2)}, u32[]{:S(2)}) collective-permute-start(f32[2,1,64,128]{2,1,3,0:T(1,128)S(1)} %get-tuple-element.16), channel_id=1, source_target_pairs={{0,4},{4,8},{8,12},{12,16},{16,20},{20,24},{24,28},{28,0},{1,5},{5... | collective-permute-start | bytes 196616 | tf_op jit(solution)/shard_map/ppermute | solution.py:18
  208.2 1.7 copy-start.6
  210.3 14.6 %copy-start.7 = (f32[8,8,64,128]{3,2,1,0:T(8,128)S(1)}, f32[8,8,64,128]{3,2,1,0:T(8,128)}, u32[]{:S(2)}) copy-start(f32[8,8,64,128]{3,2,1,0:T(8,128)} %all-gather.4.cloned.1.call-done) | copy-start | bytes 6291460
Sparse Core Ops, SparseCore 0:
  11.0 47.1 all-gather.3
